TPU v7x, 32 devices: a whole 2x2x4 slice. The times are simulated.
32 devices in a mesh: feat: 8 (over z, y), row: 2 (over x), col: 2 (over core).
Axes of the slice: x: 2, y: 2, z: 4, core: 2. Of those that a mesh axis runs over, the one named last changes fastest.
Arguments:
- local_x: float32 [4, 32, 256], P(('row', 'col'), 'feat'), may hold values from -4 to 4
- dual_var: float32 [4, 32, 256], P(('row', 'col'), 'feat'), may hold values from -2 to 2
- consensus_old: float32 [32, 256], P('feat'), may hold values from -4 to 4
- blocks_data: bfloat16 [4, 32, 512, 256], P(('row', 'col'), 'feat'), may hold values from -0.375 to 0.375
- row_index: int32 [4, 32, 512], P(('row', 'col'), 'feat'), may hold values from 0 to 16383, as said below
- labels: int32 [4, 16384], P(('row', 'col')), may hold values 0 or 1
Outputs:
- solved_x: float32 [4, 32, 256], P(('row', 'col'), 'feat')
- dual_new: float32 [4, 32, 256], P(('row', 'col'), 'feat')
- consensus: float32 [32, 256], P('feat')
- norms: float32 [2], replicated
Inputs may be any that keep to these rules, and one draw needn't show every extreme that they name: `row_index`: the 512 rows of one block are distinct samples of its shard; a sample may appear in no block or in several.
All inputs are finite; a program needn't handle non-finite values. No bound on the sum of `labels` on one device may be relied on, other than what follows from the above.
Results may differ from a plain program's by a relative error of at most 0.0019.
Values sent between devices are 32-bit elements; how exact they have to be, the bound alone decides.
A program may use at most 64 MiB of HBM per device.

v0:
```python
import jax
import jax.numpy as jnp
from jax import lax
from jax.sharding import PartitionSpec as P

NEWTON_STEPS = 2
CG_STEPS = 3
penalty = 1.0
damping = 0.5
threshold = 0.05


def shrink(values):
    return jnp.sign(values) * jnp.maximum(jnp.abs(values) - threshold, 0.0)


def conjugate_solve(hessian, gradient):
    delta = jnp.zeros_like(gradient)
    residual = gradient
    direction = gradient
    power = jnp.sum(residual * residual, axis=1)
    for cg_step in range(CG_STEPS):
        image = jnp.einsum("bkl,bl->bk", hessian, direction, precision=lax.Precision.HIGHEST)
        alpha = power / jnp.sum(direction * image, axis=1)
        delta = delta + alpha[:, None] * direction
        residual = residual - alpha[:, None] * image
        power_next = jnp.sum(residual * residual, axis=1)
        direction = residual + (power_next / power)[:, None] * direction
        power = power_next
    return delta


def local(local_x, dual_var, consensus_old, blocks_data, row_index, labels):
    iterate = local_x[0]
    dual_local = dual_var[0]
    block_rows = blocks_data[0]
    index_rows = row_index[0]
    targets = labels[0].astype(jnp.float32)
    samples = targets.shape[0]
    target = consensus_old - dual_local
    flat_index = index_rows.reshape(-1)
    identity = jnp.eye(iterate.shape[1], dtype=jnp.float32)
    for newton_step in range(NEWTON_STEPS):
        rounded = iterate.astype(jnp.bfloat16)
        partial_value = jnp.einsum(
            "brk,bk->br", block_rows, rounded, preferred_element_type=jnp.float32
        )
        local_margins = jax.ops.segment_sum(
            partial_value.reshape(-1), flat_index, num_segments=samples
        )
        margins = lax.psum(local_margins, "feat")
        prob = jax.nn.sigmoid(margins)
        misfit = prob - targets
        weights = prob * (1.0 - prob)
        misfit_rows = misfit[index_rows].astype(jnp.bfloat16)
        gradient = jnp.einsum(
            "brk,br->bk", block_rows, misfit_rows, preferred_element_type=jnp.float32
        )
        gradient = gradient + penalty * (iterate - target)
        weighted = (block_rows * weights[index_rows][:, :, None]).astype(jnp.bfloat16)
        hessian = (
            jnp.einsum("brk,brl->bkl", block_rows, weighted, preferred_element_type=jnp.float32)
            + penalty * identity
        )
        delta = conjugate_solve(hessian, gradient)
        iterate = iterate - damping * delta
    shards = lax.axis_size(("row", "col"))
    combined = iterate + dual_local
    totals = lax.psum(combined, ("row", "col"))
    consensus = shrink(totals / jnp.float32(shards))
    dual_next = dual_local + iterate - consensus
    primal_local = jnp.sum((iterate - consensus) ** 2)
    change_local = jnp.sum((consensus - consensus_old) ** 2)
    primal_total, change_total = lax.psum(
        (primal_local, change_local / jnp.float32(shards)), ("feat", "row", "col")
    )
    norms = jnp.stack(
        [jnp.sqrt(primal_total), penalty * jnp.sqrt(jnp.float32(shards) * change_total)]
    )
    return (iterate[None], dual_next[None], consensus, norms)


def solution(mesh):
    placed = (
        P(("row", "col"), "feat", None),
        P(("row", "col"), "feat", None),
        P("feat", None),
        P(("row", "col"), "feat", None, None),
        P(("row", "col"), "feat", None),
        P(("row", "col"), None),
    )
    return jax.shard_map(
        local,
        mesh=mesh,
        in_specs=placed,
        out_specs=(
            P(("row", "col"), "feat", None),
            P(("row", "col"), "feat", None),
            P("feat", None),
            P(),
        ),
        check_vma=False,
    )
```

profile of v0, /device:TPU:0, one launch (start us, length us, event | category | flops | bytes accessed | tf_op | source)
XLA Modules:
  0.0 292.5 jit_solution(3661908139111151564)
XLA Ops:
  7.2 0.0 all-reduce.4.cloned.1.call-start
  7.2 0.7 fusion.62
  7.9 1.6 fusion.26
  9.6 11.8 %scatter_custom_fusion = f32[16384]{0:T(1024)} fusion(s32[2048]{0:T(1024)S(1)} %bitcast.146, f32[2048]{0:T(1024)S(1)} %bitcast.149, f32[]{:T(128)} %constant.9.clone.1), kind=kCustom, calls=%fused_computation.36 | custom fusion | flops 2048 | bytes 65540 | tf_op jit(solution)/shard_map/scatter-add | solution.py:48
  21.4 0.0 all-reduce.4.cloned.1.call-update
  21.4 0.0 all-reduce.6.cloned.1.call-start
  21.6 72.0 %all-reduce.4.cloned.1.call-done = f32[16384]{0:T(1024)} async-done(((f32[16384]{0:T(1024)}), f32[16384]{0:T(1024)}) %all-reduce.4.cloned.1.call-update) | async-done | bytes 65552 | tf_op jit(solution)/shard_map/psum | solution.py:51
  93.5 0.9 subtract_multiply_fusion.1
  94.4 11.8 %gather_fusion.1 = f32[2048]{0:T(1024)S(1)} fusion(f32[16384]{0:T(1024)S(1)} %subtract_multiply_fusion.1, s32[2048]{0:T(1024)S(1)} %broadcast_clamp_fusion), kind=kCustom, calls=%fused_computation.1 | custom fusion | bytes 24576 | tf_op jit(solution)/shard_map/gather | solution.py:60
  106.3 13.1 %gather_fusion = bf16[2048]{0:T(1024)(128)(2,1)S(1)} fusion(bf16[16384]{0:T(1024)(128)(2,1)S(1)} %fusion.35, s32[2048]{0:T(1024)S(1)} %broadcast_clamp_fusion), kind=kCustom, calls=%fused_computation | custom fusion | bytes 16384 | tf_op jit(solution)/shard_map/gather | solution.py:55
  119.4 0.2 fusion.24
  119.7 0.9 fusion.9
  120.6 0.7 fusion.59
  121.3 0.1 fusion.46
  121.5 0.2 multiply_reduce_fusion.6
  121.7 0.1 multiply_add_fusion.3
  121.7 0.7 fusion.57
  122.4 0.1 fusion.44
  122.5 0.2 multiply_reduce_fusion.5
  122.7 0.1 multiply_add_fusion.2
  122.8 0.7 fusion.55
  123.5 0.1 fusion.43
  123.6 0.1 convert_bitcast_fusion
  123.7 0.4 fusion.20
  124.1 11.8 %scatter_custom_fusion.1 = f32[16384]{0:T(1024)} fusion(s32[2048]{0:T(1024)S(1)} %bitcast.147, f32[2048]{0:T(1024)S(1)} %bitcast.148, f32[]{:T(128)} %constant.9.clone.1), kind=kCustom, calls=%fused_computation.34 | custom fusion | flops 2048 | bytes 65540 | tf_op jit(solution)/shard_map/scatter-add | solution.py:48
  135.9 0.0 all-reduce.6.cloned.1.call-update
  135.9 69.3 %all-reduce.6.cloned.1.call-done = f32[16384]{0:T(1024)} async-done(((f32[16384]{0:T(1024)}), f32[16384]{0:T(1024)}) %all-reduce.6.cloned.1.call-update) | async-done | bytes 65552 | tf_op jit(solution)/shard_map/psum | solution.py:51
  205.3 0.9 fusion.36
  206.2 13.1 %gather_fusion.2 = bf16[2048]{0:T(1024)(128)(2,1)S(1)} fusion(bf16[16384]{0:T(1024)(128)(2,1)S(1)} %fusion.36, s32[2048]{0:T(1024)S(1)} %broadcast_clamp_fusion), kind=kCustom, calls=%fused_computation.2 | custom fusion | bytes 16384 | tf_op jit(solution)/shard_map/gather | solution.py:55
  219.3 11.8 %gather_fusion.3 = f32[2048]{0:T(1024)S(1)} fusion(f32[16384]{0:T(1024)S(1)} %subtract_multiply_fusion, s32[2048]{0:T(1024)S(1)} %broadcast_clamp_fusion), kind=kCustom, calls=%fused_computation.3 | custom fusion | bytes 24576 | tf_op jit(solution)/shard_map/gather | solution.py:60
  231.1 0.2 fusion.18
  231.3 0.9 fusion.15
  232.3 0.7 fusion.52
  233.0 0.1 fusion.41
  233.1 0.2 multiply_reduce_fusion.3
  233.3 0.1 multiply_add_fusion.1
  233.4 0.7 fusion.50
  234.1 0.1 fusion.39
  234.2 0.2 multiply_reduce_fusion.2
  234.4 0.1 multiply_add_fusion
  234.5 0.7 fusion.48
  235.1 0.1 fusion.38
  235.3 0.1 bitcast_add_fusion.1
  235.3 5.7 %psum.37 = f32[4,256]{1,0:T(4,128)S(1)} all-reduce(f32[4,256]{1,0:T(4,128)S(1)} %get-tuple-element.13), channel_id=1, replica_groups=mesh['feat'=8,'row'=2,'col'=2] {'row','col'}, use_global_device_ids=true, to_apply=%region_16.0 | all-reduce | flops 1024 | bytes 8192 | tf_op jit(solution)/shard_map/psum | solution.py:69
  241.0 0.7 multiply_reduce_fusion.1
  241.7 0.6 subtract_bitcast_fusion
  243.0 40.8 %all-reduce = (f32[]{:T(128)}, f32[]{:T(128)}) all-reduce(f32[]{:T(128)S(6)} %div.99, f32[]{:T(128)} %get-tuple-element.4), channel_id=1, replica_groups=mesh['feat'=8,'row'=2,'col'=2] {'feat','row','col'}, use_global_device_ids=true, to_apply=%region_20.0 | all-reduce | flops 2 | bytes 16 | tf_op jit(solution)/shard_map/psum | solution.py:74
  285.1 0.6 pad_maximum_fusion
  (48 shorter events, 0.3 us)
Async XLA Ops:
  7.2 2.4 copy-start.7
  7.2 14.3 %copy-start.3 = (s32[1,16384]{1,0:T(1,128)S(1)}, s32[1,16384]{1,0:T(1,128)}, u32[]{:S(2)}) copy-start(s32[1,16384]{1,0:T(1,128)} %param.11) | copy-start | bytes 196612
  7.2 86.4 %all-reduce.4.cloned.1.call-start = ((), (), s32[]{:S(2)}) async-start(), calls=%async_computation | async-start | bytes 131072 | tf_op jit(solution)/shard_map/psum | solution.py:51
  21.4 183.9 %all-reduce.6.cloned.1.call-start = ((), (), s32[]{:S(2)}) async-start(), calls=%async_computation.1 | async-start | bytes 131072 | tf_op jit(solution)/shard_map/psum | solution.py:51
  94.4 11.8 %copy-start.1 = (f32[16384]{0:T(1024)S(1)}, f32[16384]{0:T(1024)}, u32[]{:S(2)}) copy-start(f32[16384]{0:T(1024)} %all-reduce.4.cloned.1.call-done) | copy-start | bytes 196612
  106.3 13.1 %copy-start = (bf16[1,4,512,256]{3,2,1,0:T(8,128)(2,1)S(1)}, bf16[1,4,512,256]{3,2,1,0:T(8,128)(2,1)}, u32[]{:S(2)}) copy-start(bf16[1,4,512,256]{3,2,1,0:T(8,128)(2,1)} %param.9) | copy-start | bytes 3145732
  119.6 0.9 copy-start.4
  119.6 1.0 copy-start.5
  119.6 1.0 copy-start.6
  206.1 13.1 %copy-start.2 = (f32[16384]{0:T(1024)S(1)}, f32[16384]{0:T(1024)}, u32[]{:S(2)}) copy-start(f32[16384]{0:T(1024)} %all-reduce.6.cloned.1.call-done) | copy-start | bytes 196612
  235.3 50.3 %copy-start.9 = (f32[4,256]{1,0:T(4,128)}, f32[4,256]{1,0:T(4,128)S(1)}, u32[]{:S(2)}) copy-start(f32[4,256]{1,0:T(4,128)S(1)} %get-tuple-element.14) | copy-start | bytes 12292
  241.7 44.0 %copy-start.8 = (f32[4,256]{1,0:T(4,128)}, f32[4,256]{1,0:T(4,128)S(1)}, u32[]{:S(2)}) copy-start(f32[4,256]{1,0:T(4,128)S(1)} %get-tuple-element.12) | copy-start | bytes 12292
Sparse Core Ops, SparseCore 0:
  21.5 71.9 all-reduce.3
  136.0 69.1 all-reduce.5
where the time goes:
time: 293 us; the launch traced here: 292 us
  waiting for transfers between devices  141 us (48%)
  local copies, waits for them, and re-layouts  49.8 us (17%)
  blocking collectives  46.4 us (16%)
  other arithmetic  30.1 us (10%)
  between operations  16.4 us (6%)
  matrix products  8.28 us (3%)
    psum x2, waiting for transfers between devices, local(): margins = lax.psum(local_margins, 'feat')  141 us
    psum x1, blocking collectives, local(): lax.psum((primal_local, change_local / jnp.float32(shards)), ('feat', 'ro...  40.8 us
    gather x2, local copies, waits for them, and re-layouts, local(): misfit_rows = misfit[index_rows].astype(jnp.bfloat16)  26.2 us
    scatter-add x2, other arithmetic, local(): jax.ops.segment_sum(partial_value.reshape(-1), flat_index, num_segments=s...  23.7 us
    gather x4, local copies, waits for them, and re-layouts, local(): weights[index_rows][:, :, None]  23.6 us
  transfers between devices with their start and end apart: 2, of which 2 were waited for; matrix products, arithmetic and copies ran while one was open for 0% of the time, Pallas kernels for 0%

commit v1 on v0

--- a/solution.py
+++ b/solution.py
@@ -72,7 +72,7 @@
     primal_local = jnp.sum((iterate - consensus) ** 2)
     change_local = jnp.sum((consensus - consensus_old) ** 2)
     primal_total, change_total = lax.psum(
-        (primal_local, change_local / jnp.float32(shards)), ("feat", "row", "col")
+        lax.psum((primal_local, change_local / jnp.float32(shards)), "feat"), ("row", "col")
     )
     norms = jnp.stack(
         [jnp.sqrt(primal_total), penalty * jnp.sqrt(jnp.float32(shards) * change_total)]

time: 293 us -> 280 us (0.956)
  blocking collectives: 46.4 us -> 33 us
    psum x1 -> x2, blocking collectives: 40.8 us -> 27.4 us  [the longest x1 21 us: local(): lax.psum((primal_local, change_local / jnp.float32(shards)), 'feat')]
where the time goes in v1:
time: 280 us; the launch traced here: 279 us
  waiting for transfers between devices  141 us (50%)
  local copies, waits for them, and re-layouts  49.8 us (18%)
  blocking collectives  33 us (12%)
  other arithmetic  30.1 us (11%)
  between operations  16.5 us (6%)
  matrix products  8.28 us (3%)
    psum x2, waiting for transfers between devices, local(): margins = lax.psum(local_margins, 'feat')  141 us
    gather x2, local copies, waits for them, and re-layouts, local(): misfit_rows = misfit[index_rows].astype(jnp.bfloat16)  26.2 us
    scatter-add x2, other arithmetic, local(): jax.ops.segment_sum(partial_value.reshape(-1), flat_index, num_segments=s...  23.7 us
    gather x4, local copies, waits for them, and re-layouts, local(): weights[index_rows][:, :, None]  23.6 us
    psum x1, blocking collectives, local(): lax.psum((primal_local, change_local / jnp.float32(shards)), 'feat')  21 us
    psum x1, blocking collectives, local(): lax.psum(lax.psum((primal_local, change_local / jnp.float32(shards)), 'fe...  6.35 us
    psum x1, blocking collectives, local(): totals = lax.psum(combined, ('row', 'col'))  5.65 us
  transfers between devices with their start and end apart: 2, of which 2 were waited for; matrix products, arithmetic and copies ran while one was open for 0% of the time, Pallas kernels for 0%

profile of v1, /device:TPU:0, one launch (start us, length us, event | category | flops | bytes accessed | tf_op | source)
XLA Modules:
  0.0 279.2 jit_solution(10560783726298166459)
XLA Ops:
  7.2 0.0 all-reduce.5.cloned.1.call-start
  7.2 0.7 fusion.62
  7.9 1.6 fusion.26
  9.6 11.8 %scatter_custom_fusion = f32[16384]{0:T(1024)} fusion(s32[2048]{0:T(1024)S(1)} %bitcast.146, f32[2048]{0:T(1024)S(1)} %bitcast.149, f32[]{:T(128)} %constant.9.clone.1), kind=kCustom, calls=%fused_computation.36 | custom fusion | flops 2048 | bytes 65540 | tf_op jit(solution)/shard_map/scatter-add | solution.py:48
  21.4 0.0 all-reduce.5.cloned.1.call-update
  21.4 0.0 all-reduce.7.cloned.1.call-start
  21.6 72.0 %all-reduce.5.cloned.1.call-done = f32[16384]{0:T(1024)} async-done(((f32[16384]{0:T(1024)}), f32[16384]{0:T(1024)}) %all-reduce.5.cloned.1.call-update) | async-done | bytes 65552 | tf_op jit(solution)/shard_map/psum | solution.py:51
  93.5 0.9 subtract_multiply_fusion.1
  94.4 11.8 %gather_fusion.1 = f32[2048]{0:T(1024)S(1)} fusion(f32[16384]{0:T(1024)S(1)} %subtract_multiply_fusion.1, s32[2048]{0:T(1024)S(1)} %broadcast_clamp_fusion), kind=kCustom, calls=%fused_computation.1 | custom fusion | bytes 24576 | tf_op jit(solution)/shard_map/gather | solution.py:60
  106.3 13.1 %gather_fusion = bf16[2048]{0:T(1024)(128)(2,1)S(1)} fusion(bf16[16384]{0:T(1024)(128)(2,1)S(1)} %fusion.35, s32[2048]{0:T(1024)S(1)} %broadcast_clamp_fusion), kind=kCustom, calls=%fused_computation | custom fusion | bytes 16384 | tf_op jit(solution)/shard_map/gather | solution.py:55
  119.4 0.2 fusion.24
  119.7 0.9 fusion.9
  120.6 0.7 fusion.59
  121.3 0.1 fusion.46
  121.5 0.2 multiply_reduce_fusion.6
  121.7 0.1 multiply_add_fusion.3
  121.7 0.7 fusion.57
  122.4 0.1 fusion.44
  122.5 0.2 multiply_reduce_fusion.5
  122.7 0.1 multiply_add_fusion.2
  122.8 0.7 fusion.55
  123.5 0.1 fusion.43
  123.6 0.1 convert_bitcast_fusion
  123.7 0.4 fusion.20
  124.1 11.8 %scatter_custom_fusion.1 = f32[16384]{0:T(1024)} fusion(s32[2048]{0:T(1024)S(1)} %bitcast.147, f32[2048]{0:T(1024)S(1)} %bitcast.148, f32[]{:T(128)} %constant.9.clone.1), kind=kCustom, calls=%fused_computation.34 | custom fusion | flops 2048 | bytes 65540 | tf_op jit(solution)/shard_map/scatter-add | solution.py:48
  135.9 69.3 %all-reduce.7.cloned.1.call-done = f32[16384]{0:T(1024)} async-done(((f32[16384]{0:T(1024)}), f32[16384]{0:T(1024)}) %all-reduce.7.cloned.1.call-update) | async-done | bytes 65552 | tf_op jit(solution)/shard_map/psum | solution.py:51
  205.3 0.9 fusion.36
  206.2 13.1 %gather_fusion.2 = bf16[2048]{0:T(1024)(128)(2,1)S(1)} fusion(bf16[16384]{0:T(1024)(128)(2,1)S(1)} %fusion.36, s32[2048]{0:T(1024)S(1)} %broadcast_clamp_fusion), kind=kCustom, calls=%fused_computation.2 | custom fusion | bytes 16384 | tf_op jit(solution)/shard_map/gather | solution.py:55
  219.3 11.8 %gather_fusion.3 = f32[2048]{0:T(1024)S(1)} fusion(f32[16384]{0:T(1024)S(1)} %subtract_multiply_fusion, s32[2048]{0:T(1024)S(1)} %broadcast_clamp_fusion), kind=kCustom, calls=%fused_computation.3 | custom fusion | bytes 24576 | tf_op jit(solution)/shard_map/gather | solution.py:60
  231.1 0.2 fusion.18
  231.3 0.9 fusion.15
  232.3 0.7 fusion.52
  233.0 0.1 fusion.41
  233.1 0.2 multiply_reduce_fusion.3
  233.3 0.1 multiply_add_fusion.1
  233.4 0.7 fusion.50
  234.1 0.1 fusion.39
  234.2 0.2 multiply_reduce_fusion.2
  234.4 0.1 multiply_add_fusion
  234.5 0.7 fusion.48
  235.1 0.1 fusion.38
  235.3 0.1 bitcast_add_fusion.1
  235.3 5.7 %psum.51 = f32[4,256]{1,0:T(4,128)S(1)} all-reduce(f32[4,256]{1,0:T(4,128)S(1)} %get-tuple-element.15), channel_id=1, replica_groups=mesh['feat'=8,'row'=2,'col'=2] {'row','col'}, use_global_device_ids=true, to_apply=%region_16.0 | all-reduce | flops 1024 | bytes 8192 | tf_op jit(solution)/shard_map/psum | solution.py:69
  241.0 0.7 multiply_reduce_fusion.1
  241.7 0.6 subtract_bitcast_fusion
  243.0 21.0 %all-reduce = (f32[]{:T(128)}, f32[]{:T(128)}) all-reduce(f32[]{:T(128)S(6)} %div.99, f32[]{:T(128)} %get-tuple-element.4), channel_id=1, replica_groups=mesh['feat'=8,'row'=2,'col'=2] {'feat'}, use_global_device_ids=true, to_apply=%region_21.0 | all-reduce | flops 2 | bytes 16 | tf_op jit(solution)/shard_map/psum | solution.py:75
  264.0 6.3 %all-reduce.1 = (f32[]{:T(128)}, f32[]{:T(128)}) all-reduce(f32[]{:T(128)} %get-tuple-element.10, f32[]{:T(128)} %get-tuple-element.11), channel_id=1, replica_groups=mesh['feat'=8,'row'=2,'col'=2] {'row','col'}, use_global_device_ids=true, to_apply=%region_22.0 | all-reduce | flops 2 | bytes 16 | tf_op jit(solution)/shard_map/psum | solution.py:74
  271.8 0.6 pad_maximum_fusion
  (49 shorter events, 0.4 us)
Async XLA Ops:
  7.2 2.4 copy-start.7
  7.2 14.3 %copy-start.3 = (s32[1,16384]{1,0:T(1,128)S(1)}, s32[1,16384]{1,0:T(1,128)}, u32[]{:S(2)}) copy-start(s32[1,16384]{1,0:T(1,128)} %param.11) | copy-start | bytes 196612
  7.2 86.4 %all-reduce.5.cloned.1.call-start = ((), (), s32[]{:S(2)}) async-start(), calls=%async_computation | async-start | bytes 131072 | tf_op jit(solution)/shard_map/psum | solution.py:51
  21.4 183.9 %all-reduce.7.cloned.1.call-start = ((), (), s32[]{:S(2)}) async-start(), calls=%async_computation.1 | async-start | bytes 131072 | tf_op jit(solution)/shard_map/psum | solution.py:51
  94.4 11.8 %copy-start.1 = (f32[16384]{0:T(1024)S(1)}, f32[16384]{0:T(1024)}, u32[]{:S(2)}) copy-start(f32[16384]{0:T(1024)} %all-reduce.5.cloned.1.call-done) | copy-start | bytes 196612
  106.3 13.1 %copy-start = (bf16[1,4,512,256]{3,2,1,0:T(8,128)(2,1)S(1)}, bf16[1,4,512,256]{3,2,1,0:T(8,128)(2,1)}, u32[]{:S(2)}) copy-start(bf16[1,4,512,256]{3,2,1,0:T(8,128)(2,1)} %param.9) | copy-start | bytes 3145732
  119.6 0.9 copy-start.4
  119.6 1.0 copy-start.5
  119.6 1.0 copy-start.6
  206.1 13.1 %copy-start.2 = (f32[16384]{0:T(1024)S(1)}, f32[16384]{0:T(1024)}, u32[]{:S(2)}) copy-start(f32[16384]{0:T(1024)} %all-reduce.7.cloned.1.call-done) | copy-start | bytes 196612
  235.3 37.0 %copy-start.9 = (f32[4,256]{1,0:T(4,128)}, f32[4,256]{1,0:T(4,128)S(1)}, u32[]{:S(2)}) copy-start(f32[4,256]{1,0:T(4,128)S(1)} %get-tuple-element.16) | copy-start | bytes 12292
  241.7 30.7 %copy-start.8 = (f32[4,256]{1,0:T(4,128)}, f32[4,256]{1,0:T(4,128)S(1)}, u32[]{:S(2)}) copy-start(f32[4,256]{1,0:T(4,128)S(1)} %get-tuple-element.14) | copy-start | bytes 12292
Sparse Core Ops, SparseCore 0:
  21.5 71.9 all-reduce.4
  136.0 69.1 all-reduce.6
